TPU v7x, 256 devices: a whole 4x4x8 slice. The times are simulated.
256 devices in a mesh: strip: 32 (over z, x), col: 8 (over y, core).
Axes of the slice: x: 4, y: 4, z: 8, core: 2. Of those that a mesh axis runs over, the one named last changes fastest.
Arguments:
- residuals: float32 [64, 64, 2560], P('strip'), may hold values from -6 to 6
- corr_rows: float32 [64], replicated, may hold values from 0.5 to 2
- corr_cols: float32 [2560], replicated, may hold values from 0.5 to 2
- row_anchor: int32 [64], replicated, may hold values from 0 to 448
- col_anchor: int32 [64], replicated, may hold values from 0 to 17920
- valid_first: int32 [64], replicated, may hold values from 0 to 15
- valid_end: int32 [64], replicated, may hold values from 49 to 64
- facet_of_slot: int32 [64], replicated, may hold values from 0 to 63, each once
Outputs:
- stitched: float32 [512, 20480], P('strip', 'col')
- column_power: float32 [20480], P('col')
Inputs may be any that keep to these rules, and one draw needn't show every extreme that they name: facet_of_slot names each of the 64 facets exactly once.
All inputs are finite; a program needn't handle non-finite values.
Results may differ from a plain program's by a relative error of at most 0.0003.
Values sent between devices are 32-bit elements; how exact they have to be, the bound alone decides.
A program may use at most 64 MiB of HBM per device.

v0:
```python
from functools import reduce

import jax
import jax.numpy as jnp
from jax import lax
from jax.sharding import PartitionSpec as P


def copy_for_each(shard, axis):
    copies = jnp.broadcast_to(shard, (lax.axis_size(axis), *shard.shape))
    return lax.all_to_all(copies, axis, split_axis=0, concat_axis=0, tiled=True)


def taken_together(shard, axis):
    return copy_for_each(shard, axis).sum(axis=0)


def tapers(count):
    position = (jnp.arange(count).astype(jnp.float32) + 0.5) / count
    return jnp.sin(jnp.pi * position) ** 2


def body(
    residuals, corr_rows, corr_cols, row_anchor, col_anchor, valid_first, valid_end, facet_of_slot
):
    local_count, facet_rows, facet_cols = residuals.shape
    strip_count = lax.axis_size("strip")
    strip_rows = facet_rows // 4
    image_rows = strip_count * strip_rows
    strip_index = lax.axis_index("strip")
    group_index = lax.axis_index("col")
    row_index = jnp.arange(facet_rows)
    row_taper = tapers(facet_rows)
    col_taper = tapers(facet_cols)
    correction = corr_rows[:, None] * corr_cols[None, :]
    side_blank = jnp.zeros((facet_rows, facet_cols), jnp.float32)
    num_bands = []
    for position in range(local_count):
        facet_id = facet_of_slot[strip_index * local_count + position]
        inside = (row_index >= valid_first[facet_id]) & (row_index < valid_end[facet_id])
        row_weight = jnp.where(inside, row_taper, 0.0)
        weight = row_weight[:, None] * col_taper[None, :]
        col_start = jnp.clip(
            group_index * facet_cols - col_anchor[facet_id] + facet_cols, 0, 2 * facet_cols
        )
        padded = jnp.concatenate(
            [side_blank, weight * correction * residuals[position], side_blank], axis=1
        )
        shifted = lax.dynamic_slice_in_dim(padded, col_start, facet_cols, 1)
        canvas = jnp.zeros((image_rows, facet_cols), jnp.float32)
        canvas = lax.dynamic_update_slice(canvas, shifted, (row_anchor[facet_id], 0))
        num_bands.append(canvas.reshape(strip_count, strip_rows, facet_cols))
    num_send = reduce(jnp.add, num_bands)[:, None]
    got_num = lax.all_to_all(num_send, "strip", split_axis=0, concat_axis=0, tiled=True)
    facet_ids = jnp.arange(facet_of_slot.shape[0])
    row_local = strip_index * strip_rows + jnp.arange(strip_rows)
    row_pos = row_local[None, :] - row_anchor[:, None]
    row_inside = (row_pos >= valid_first[:, None]) & (row_pos < valid_end[:, None])
    row_value = jnp.sin(jnp.pi * (row_pos.astype(jnp.float32) + 0.5) / facet_rows) ** 2
    row_part = jnp.where(row_inside, row_value, 0.0)
    col_local = group_index * facet_cols + jnp.arange(facet_cols)
    col_pos = col_local[None, :] - col_anchor[facet_ids][:, None]
    col_inside = (col_pos >= 0) & (col_pos < facet_cols)
    col_value = jnp.sin(jnp.pi * (col_pos.astype(jnp.float32) + 0.5) / facet_cols) ** 2
    col_part = jnp.where(col_inside, col_value, 0.0)
    denominator = jnp.einsum("fv,fu->vu", row_part, col_part, precision=lax.Precision.HIGHEST)
    numerator = jnp.sum(got_num, axis=(0, 1))
    stitched = numerator / jnp.maximum(denominator, 0.5)
    column_sums = taken_together(jnp.sum(stitched * stitched, axis=0), "strip")
    return (stitched, column_sums / image_rows)


def solution(mesh):
    in_specs = (P("strip", None, None), P(), P(), P(), P(), P(), P(), P())
    out_specs = (P("strip", "col"), P("col"))
    return jax.shard_map(body, mesh=mesh, in_specs=in_specs, out_specs=out_specs, check_vma=False)
```

profile of v0, /device:TPU:1, one launch (start us, length us, event | category | flops | bytes accessed | tf_op | source)
XLA Modules:
  0.0 187.9 jit_solution(4750601892340826790)
XLA Ops:
  0.6 1.3 fusion.48
  4.6 0.1 sine_multiply_fusion
  5.9 1.4 fusion.44
  9.8 1.4 fusion.46
  12.5 1.2 and_select_fusion
  13.7 1.3 and_select_fusion.1
  16.3 1.5 fusion.2
  17.9 0.6 fusion.13
  18.5 3.0 %broadcast.76 = f32[512,2560]{1,0:T(8,128)} broadcast(f32[]{:T(128)} %constant.17.clone.1), dimensions={} | broadcast | bytes 5242884 | tf_op jit(solution)/shard_map/broadcast.1
  21.5 3.1 %dynamic_update_slice.8 = f32[512,2560]{1,0:T(8,128)} dynamic-update-slice(f32[512,2560]{1,0:T(8,128)} %broadcast.76, f32[64,2560]{1,0:T(8,128)S(1)} %fusion.13, s32[]{:T(128)S(6)} %select_n.53, s32[]{:T(128)} %constant.21.clone.1) | dynamic-update-slice | bytes 1310724 | tf_op jit(solution)/shard_map/dynamic_update_slice | solution.py:51
  24.6 1.7 fusion.11
  26.3 3.1 %add.125 = f32[512,2560]{1,0:T(8,128)} dynamic-update-slice(f32[512,2560]{1,0:T(8,128)} %dynamic_update_slice.8, f32[64,2560]{1,0:T(8,128)S(1)} %fusion.11, s32[]{:T(128)S(6)} %select_n.56, s32[]{:T(128)} %constant.21.clone.1) | dynamic-update-slice | bytes 1310724 | tf_op jit(solution)/shard_map/add | solution.py:53
  29.4 0.0 copy-start
  29.4 12.1 %all-to-all-start = ((f32[32,1,16,2560]{3,2,1,0:T(8,128)}), f32[32,1,16,2560]{3,2,1,0:T(8,128)}, u32[]{:S(2)}, u32[]{:S(2)}) async-start(f32[32,1,16,2560]{3,2,1,0:T(8,128)} %bitcast.15), calls=%async_computation | async-start | bytes 10485760 | tf_op jit(solution)/shard_map/all_to_all | solution.py:54
  41.5 0.0 copy-done
  41.5 0.8 gather_fusion
  42.3 0.0 copy-start.1
  42.3 0.0 copy-start.2
  42.3 0.0 copy-start.3
  42.3 113.8 %all-to-all-done = f32[32,1,16,2560]{3,2,1,0:T(8,128)} async-done(((f32[32,1,16,2560]{3,2,1,0:T(8,128)}), f32[32,1,16,2560]{3,2,1,0:T(8,128)}, u32[]{:S(2)}, u32[]{:S(2)}) %all-to-all-start) | async-done | bytes 5242912 | tf_op jit(solution)/shard_map/all_to_all | solution.py:54
  156.1 2.7 %reduce_sum.27 = f32[16,2560]{1,0:T(8,128)S(1)} reduce(f32[32,1,16,2560]{3,2,1,0:T(8,128)} %all-to-all-done, f32[]{:T(128)} %constant.17.clone.1), dimensions={0,1}, to_apply=%region_0.1 | reduce | flops 1269760 | bytes 5406724 | tf_op jit(solution)/shard_map/reduce_sum | solution.py:67
  158.9 0.0 copy-done.1
  158.9 0.0 copy-done.2
  158.9 0.0 copy-done.3
  158.9 3.5 %multiply_reduce_fusion = (f32[2560]{0:T(1024)S(1)}, f32[16,2560]{1,0:T(8,128)}) fusion(f32[16,2560]{1,0:T(8,128)S(1)} %reduce_sum.27, s32[64]{0:T(128)S(1)} %gather_fusion, s32[2560]{0:T(1024)S(1)} %iota_add_fusion, s32[64]{0:T(128)S(1)} %copy-done.1, s32[64]{0:T(128)S(1)} %copy-done.3, s32[64]{0:T(128)S(1)} %copy-done.2, s32[16]{0:T(128)S(1)} %iota_add_fusion.1), kind=kOutput, calls=%fused_computation.34 | convolution fusion | flops 33102336 | bytes 349248 | tf_op jit(solution)/shard_map/fv,fu->vu/dot_general | solution.py:66
  162.4 0.2 broadcast_in_dim.17
  162.6 24.5 %all_to_all.11 = f32[32,1,2560]{2,1,0:T(1,128)S(1)} all-to-all(f32[32,1,2560]{2,1,0:T(1,128)S(1)} %broadcast_in_dim.17), channel_id=1, replica_groups=mesh['strip'=32,'col'=8] {'strip'}, dimensions={0} | all-to-all | bytes 655360 | tf_op jit(solution)/shard_map/all_to_all | solution.py:11
  187.1 0.2 reduce_sum.29
  187.3 0.6 broadcast_multiply_fusion
  (5 shorter events, 0.1 us)
Async XLA Ops:
  29.4 12.1 %copy-start = (s32[64]{0:T(128)S(1)}, s32[64]{0:T(128)}, u32[]{:S(2)}) copy-start(s32[64]{0:T(128)} %param.12) | copy-start | bytes 772
  29.4 126.8 %all-to-all-start = ((f32[32,1,16,2560]{3,2,1,0:T(8,128)}), f32[32,1,16,2560]{3,2,1,0:T(8,128)}, u32[]{:S(2)}, u32[]{:S(2)}) async-start(f32[32,1,16,2560]{3,2,1,0:T(8,128)} %bitcast.15), calls=%async_computation | async-start | bytes 10485760 | tf_op jit(solution)/shard_map/all_to_all | solution.py:54
  42.3 116.6 %copy-start.1 = (s32[64]{0:T(128)S(1)}, s32[64]{0:T(128)}, u32[]{:S(2)}) copy-start(s32[64]{0:T(128)} %param.14) | copy-start | bytes 772
  42.3 116.6 %copy-start.2 = (s32[64]{0:T(128)S(1)}, s32[64]{0:T(128)}, u32[]{:S(2)}) copy-start(s32[64]{0:T(128)} %param.11) | copy-start | bytes 772
  42.3 116.6 %copy-start.3 = (s32[64]{0:T(128)S(1)}, s32[64]{0:T(128)}, u32[]{:S(2)}) copy-start(s32[64]{0:T(128)} %param.13) | copy-start | bytes 772
where the time goes:
time: 189 us; the launch traced here: 188 us
  waiting for transfers between devices  114 us (60%)
  blocking collectives  24.5 us (13%)
  local copies, waits for them, and re-layouts  14.3 us (8%)
  starting transfers between devices  12.1 us (6%)
  other arithmetic  10 us (5%)
  between operations  9.66 us (5%)
  matrix products  3.54 us (2%)
    all_to_all x1, waiting for transfers between devices, body(): lax.all_to_all(num_send, 'strip', split_axis=0, concat_axis=0, tiled=True)  114 us
    all_to_all x1, blocking collectives, copy_for_each(): return lax.all_to_all(copies, axis, split_axis=0, concat_axis=0, tiled=True)  24.5 us
    all_to_all x1, starting transfers between devices, body(): lax.all_to_all(num_send, 'strip', split_axis=0, concat_axis=0, tiled=True)  12.1 us
  transfers between devices with their start and end apart: 1, of which 1 were waited for; matrix products, arithmetic and copies ran while one was open for 0% of the time, Pallas kernels for 0%

commit v1 on v0

v1 whole, which is shorter than its diff:
```python
import jax
import jax.numpy as jnp
from jax import lax
from jax.experimental import pallas as pl
from jax.experimental.pallas import tpu as pltpu
from jax.sharding import PartitionSpec as P


MESH = pl.DeviceIdType.MESH
FH, FW, SLOTS, ROWS, QUARTER, LANES = 64, 2560, 64, 16, 640, 128
STRIPS, COLS, ZS, XS = 32, 8, 8, 4


def squared_sine(position, count):
    return jnp.sin(jnp.pi * ((position.astype(jnp.float32) + 0.5) / count)) ** 2


def parts_of(value):
    first = value.astype(jnp.bfloat16)
    rest = value - first.astype(jnp.float32)
    second = rest.astype(jnp.bfloat16)
    third = (rest - second.astype(jnp.float32)).astype(jnp.bfloat16)
    return first, second, third


def binned(one_hot, upper, value):
    placed = jnp.concatenate([jnp.where(upper, value, 0.0), jnp.where(upper, 0.0, value)], axis=0)
    total = None
    for part in parts_of(placed):
        product = jnp.dot(one_hot, part, preferred_element_type=jnp.float32)
        total = product if total is None else total + product
    return total


def wait_for(ref, sem):
    pltpu.make_async_copy(ref, ref, sem).wait()


def kernel(
    res_hbm, crow, ccol, fos_v, ra_v, ca_v, vf_v, ve_v, fos_s, ra_s, ca_s, vf_s, ve_s,
    out, power,
    data, rowfac, colfac, turned, send1, recv1, tile, psum, pgot, psend, pall,
    load_sem, s1, r1, s2, r2, s3, r3, s4, r4,
):
    strip = lax.axis_index("strip")
    col = lax.axis_index("col")
    z, x = strip // XS, strip % XS
    y, core = col // 2, col % 2

    load = pltpu.make_async_copy(res_hbm, data, load_sem)
    load.start()

    barrier = pltpu.get_barrier_semaphore()

    def greet(peer_strip, peer_col):
        pl.semaphore_signal(barrier, inc=1, device_id=(peer_strip, peer_col), device_id_type=MESH)

    @pl.loop(1, STRIPS)
    def _(step):
        greet((strip + step) % STRIPS, col)

    @pl.loop(0, ZS * (COLS - 1))
    def _(step):
        greet(((z + step // (COLS - 1)) % ZS) * XS + x, (col + 1 + step % (COLS - 1)) % COLS)

    @pl.loop(1, XS)
    def _(step):
        greet(z * XS + (x + step) % XS, 2 * y + 1 - core)

    diagonal = lax.broadcasted_iota(jnp.int32, (SLOTS, SLOTS), 0) == lax.broadcasted_iota(jnp.int32, (SLOTS, SLOTS), 1)

    def upright(row):
        return jnp.sum(jnp.where(diagonal, row, 0.0), axis=1, keepdims=True)

    row_index = lax.broadcasted_iota(jnp.int32, (FH, LANES), 0)
    row_base = squared_sine(row_index, FH) * upright(crow[...])
    colfac[...] = squared_sine(lax.broadcasted_iota(jnp.int32, (8, FW), 1), FW) * ccol[...]
    facets = []
    for i in range(2):
        facet = fos_s[2 * strip + i]
        inside = (row_index >= vf_s[facet]) & (row_index < ve_s[facet])
        rowfac[i] = jnp.where(inside, row_base, 0.0)
        facets.append((ra_s[facet], ca_s[facet]))
    load.wait()

    sub = lax.broadcasted_iota(jnp.int32, (8, LANES), 0)
    lane = lax.broadcasted_iota(jnp.int32, (8, LANES), 1)
    for i in range(2):
        row_anchor, col_anchor = facets[i]
        first_row = lax.rem(8 * core + 448 - row_anchor, FH)
        first_col = lax.rem(QUARTER * y + 17920 - col_anchor, FW)
        group, row_off = lax.div(first_row, 8), lax.rem(first_row, 8)
        column, col_off = lax.div(first_col, LANES), lax.rem(first_col, LANES)
        row_roll, col_roll = lax.rem(8 - row_off, 8), lax.rem(LANES - col_off, LANES)
        in_first_row, in_first_col = sub < 8 - row_off, lane < LANES - col_off
        group, column = jnp.full((8, LANES), group), jnp.full((8, LANES), column)
        for k in range(8):
            row_factor = rowfac[i, 8 * k : 8 * k + 8, :]
            tiles = []
            for n in range(FW // LANES):
                part = pl.ds(LANES * n, LANES)
                tiles.append(data[i, pl.ds(8 * k, 8), part] * (row_factor * colfac[:, part]))
            for bit, count in ((16, 20), (8, 13), (4, 9), (2, 7), (1, 6)):
                moved = (column & bit) != 0
                tiles = [jnp.where(moved, tiles[(n + bit) % len(tiles)], tiles[n]) for n in range(count)]
            tiles = [pltpu.roll(tile_n, col_roll, 1) for tile_n in tiles]
            for n in range(5):
                turned[k, :, LANES * n : LANES * (n + 1)] = jnp.where(in_first_col, tiles[n], tiles[n + 1])
        for n in range(5):
            part = pl.ds(LANES * n, LANES)
            rows = [turned[k, :, part] for k in range(8)]
            for bit in (4, 2, 1):
                moved = (group & bit) != 0
                rows = [jnp.where(moved, rows[(k + bit) % 8], rows[k]) for k in range(8)]
            rows = [pltpu.roll(row_k, row_roll, 0) for row_k in rows]
            for xq in range(XS):
                send1[xq, :, i, part] = jnp.where(in_first_row, rows[2 * xq], rows[2 * xq + 1])

    pl.semaphore_wait(barrier, 90)

    @pl.loop(1, STRIPS)
    def _(step):
        peer = (strip + step) % STRIPS
        pltpu.make_async_remote_copy(
            src_ref=send1.at[peer % XS, peer // XS], dst_ref=recv1.at[strip], send_sem=s1, recv_sem=r1,
            device_id=(peer, col), device_id_type=MESH,
        ).start()

    pltpu.make_async_copy(send1.at[x, z], recv1.at[strip], r1).start()

    m = 16 * x + 8 * core + z
    facet_of = upright(fos_v[...].astype(jnp.float32)).astype(jnp.int32)
    chosen = facet_of == lax.broadcasted_iota(jnp.int32, (SLOTS, SLOTS), 1)

    def by_slot(row):
        return jnp.sum(jnp.where(chosen, row.astype(jnp.float32), 0.0), axis=1, keepdims=True).astype(jnp.int32)

    ra, ca, vf, ve = (by_slot(ref[...]) for ref in (ra_v, ca_v, vf_v, ve_v))
    block = (ra >> 6) + (m < (ra & 63)).astype(jnp.int32)
    facet_row = (m - ra) & 63
    row_weight = jnp.where((facet_row >= vf) & (facet_row < ve), squared_sine(facet_row, FH), 0.0)
    column_group = sum((ca >= FW * k).astype(jnp.int32) for k in range(1, COLS))
    first_class = ca - FW * column_group
    class_index = QUARTER * y + lax.broadcasted_iota(jnp.int32, (SLOTS, QUARTER), 1)
    upper = class_index >= first_class
    facet_col = class_index - first_class + jnp.where(upper, 0, FW)
    weight = row_weight * squared_sine(facet_col, FW)
    wide_lane = lax.broadcasted_iota(jnp.int32, (SLOTS, 2 * SLOTS), 1)
    wide_sub = lax.broadcasted_iota(jnp.int32, (SLOTS, 2 * SLOTS), 0)
    low_bin = (8 * block + column_group).astype(jnp.float32)
    bin_row = jnp.sum(jnp.where((wide_lane & 63) == wide_sub, low_bin, 0.0), axis=0, keepdims=True)
    bin_row = bin_row.astype(jnp.int32) + (wide_lane[:1] >> 6)
    one_hot = (wide_sub == bin_row).astype(jnp.float32).astype(jnp.bfloat16)
    scale = 1.0 / jnp.maximum(binned(one_hot, upper, weight), 0.5)

    wait_for(recv1, r1)
    stitched = binned(one_hot, upper, recv1[...].reshape(SLOTS, QUARTER)) * scale
    tile[...] = stitched
    squares = stitched * stitched
    sums = squares[0:8]
    for q in range(1, 8):
        sums = sums + squares[8 * q : 8 * q + 8]
    psum[0] = sums[0:4]
    psum[1] = sums[4:8]

    place = 2 * x + core

    @pl.loop(1, 8)
    def _(step):
        peer = (place + step) % 8
        pltpu.make_async_remote_copy(
            src_ref=psum.at[peer % 2], dst_ref=pgot.at[place], send_sem=s3, recv_sem=r3,
            device_id=(z * XS + peer // 2, 2 * y + peer % 2), device_id_type=MESH,
        ).start()

    pltpu.make_async_copy(psum.at[core], pgot.at[place], r3).start()

    own_bin = 8 * z + col
    out_row = 8 * core + z
    out_cols = pl.ds(pl.multiple_of(QUARTER * y, LANES), QUARTER)

    @pl.loop(1, 64)
    def _(step):
        peer = (own_bin + step) % 64
        pltpu.make_async_remote_copy(
            src_ref=tile.at[peer], dst_ref=out.at[out_row, out_cols], send_sem=s2, recv_sem=r2,
            device_id=((peer // 8) * XS + x, peer % 8), device_id_type=MESH,
        ).start()

    pltpu.make_async_copy(tile.at[own_bin], out.at[out_row, out_cols], r2).start()

    wait_for(pgot, r3)
    total = pgot[0]
    for k in range(1, 8):
        total = total + pgot[k]
    psend[...] = total

    @pl.loop(0, 32)
    def _(step):
        peer_z = (z + step // 4) % ZS
        peer_col = 4 * core + step % 4
        own = (step < 4) & (peer_col == col)

        @pl.when(own)
        def _():
            pltpu.make_async_copy(psend.at[step % 4], pall.at[z, out_cols], r4).start()

        @pl.when(jnp.logical_not(own))
        def _():
            pltpu.make_async_remote_copy(
                src_ref=psend.at[step % 4], dst_ref=pall.at[z, out_cols], send_sem=s4, recv_sem=r4,
                device_id=(peer_z * XS + x, peer_col), device_id_type=MESH,
            ).start()

    wait_for(pall, r4)
    power[...] = jnp.sum(pall[...], axis=0, keepdims=True) / (FH * 8)
    wait_for(out, r2)

    wait_for(recv1.at[pl.ds(0, STRIPS - 1)], s1)
    wait_for(pgot.at[pl.ds(0, 7)], s3)

    @pl.loop(1, 64)
    def _(step):
        wait_for(tile.at[0], s2)

    @pl.loop(0, 32)
    def _(step):
        @pl.when(jnp.logical_not((step < 4) & (4 * core + step % 4 == col)))
        def _():
            wait_for(psend.at[0], s4)


def body(residuals, corr_rows, corr_cols, row_anchor, col_anchor, valid_first, valid_end, facet_of_slot):
    ints = (facet_of_slot, row_anchor, col_anchor, valid_first, valid_end)
    vmem = pl.BlockSpec(memory_space=pltpu.VMEM)
    smem = pl.BlockSpec(memory_space=pltpu.SMEM)
    f32 = jnp.float32
    dma = pltpu.SemaphoreType.DMA
    stitched, power = pl.pallas_call(
        kernel,
        out_shape=(jax.ShapeDtypeStruct((ROWS, FW), f32), jax.ShapeDtypeStruct((1, FW), f32)),
        in_specs=[pl.BlockSpec(memory_space=pl.ANY)] + [vmem] * 7 + [smem] * 5,
        out_specs=(vmem, vmem),
        scratch_shapes=[
            pltpu.VMEM((2, FH, FW), f32),
            pltpu.VMEM((2, FH, LANES), f32),
            pltpu.VMEM((8, FW), f32),
            pltpu.VMEM((8, 8, QUARTER), f32),
            pltpu.VMEM((XS, ZS, 2, QUARTER), f32),
            pltpu.VMEM((STRIPS, 2, QUARTER), f32),
            pltpu.VMEM((64, QUARTER), f32),
            pltpu.VMEM((2, 4, QUARTER), f32),
            pltpu.VMEM((8, 4, QUARTER), f32),
            pltpu.VMEM((4, QUARTER), f32),
            pltpu.VMEM((ZS, FW), f32),
        ]
        + [dma] * 9,
        compiler_params=pltpu.CompilerParams(collective_id=0, has_side_effects=True),
        name="restitch",
    )(
        residuals, corr_rows.reshape(1, FH), corr_cols.reshape(1, FW),
        *(a.reshape(1, SLOTS) for a in ints), *ints,
    )
    return stitched, power.reshape(FW)


def solution(mesh):
    in_specs = (P("strip", None, None), P(), P(), P(), P(), P(), P(), P())
    out_specs = (P("strip", "col"), P("col"))
    return jax.shard_map(body, mesh=mesh, in_specs=in_specs, out_specs=out_specs, check_vma=False)
```

time: 189 us -> 39 us (0.21)
  waiting for transfers between devices: 114 us -> 0 us
  Pallas kernels: 0 us -> 33.9 us
  blocking collectives: 24.5 us -> 0 us
  starting transfers between devices: 12.1 us -> 0 us
  local copies, waits for them, and re-layouts: 14.3 us -> 2.91 us
  between operations: 9.66 us -> 0.64 us
  other arithmetic: 10 us -> 1.33 us
  matrix products: 3.54 us -> 0 us
    all_to_all x1 -> x0, waiting for transfers between devices: 114 us -> none  [body(): lax.all_to_all(num_send, 'strip', split_axis=0, concat_axis=0, tiled=True)]
    pallas_call x0 -> x1, Pallas kernels: none -> 33.9 us  [body(): pl.pallas_call(kernel, out_shape=(jax.ShapeDtypeStruct((ROWS, FW), f32),...]
    all_to_all x1 -> x0, blocking collectives: 24.5 us -> none  [copy_for_each(): return lax.all_to_all(copies, axis, split_axis=0, concat_axis=0, tiled=True)]
    all_to_all x1 -> x0, starting transfers between devices: 12.1 us -> none  [body(): lax.all_to_all(num_send, 'strip', split_axis=0, concat_axis=0, tiled=True)]
    dynamic_slice x3 -> x0, local copies, waits for them, and re-layouts: 4.14 us -> none  [the longest x1 1.41 us: body(): valid_end[facet_id]]
    dot_general x1 -> x0, matrix products: 3.54 us -> none  [body(): jnp.einsum('fv,fu->vu', row_part, col_part, precision=lax.Precision.HIGHEST)]
    add x1 -> x0, local copies, waits for them, and re-layouts: 3.09 us -> none  [body(): num_send = reduce(jnp.add, num_bands)[:, None]]
    dynamic_update_slice x1 -> x0, local copies, waits for them, and re-layouts: 3.08 us -> none  [body(): lax.dynamic_update_slice(canvas, shifted, (row_anchor[facet_id], 0))]
  transfers between devices with their start and end apart: 1 -> 0, of which waited for: 1 -> 0; matrix products, arithmetic and copies ran while one was open for 0% -> 0% of each run, Pallas kernels for 0% -> 0%
where the time goes in v1:
time: 39 us; the launch traced here: 38.7 us
  Pallas kernels  33.9 us (87%)
  local copies, waits for them, and re-layouts  2.91 us (7%)
  other arithmetic  1.33 us (3%)
  between operations  0.64 us (2%)
    pallas_call x1, Pallas kernels, body(): pl.pallas_call(kernel, out_shape=(jax.ShapeDtypeStruct((ROWS, FW), f32),...  33.9 us
    unnamed x1, local copies, waits for them, and re-layouts  1.59 us
    pallas_call x1, other arithmetic, body(): pl.pallas_call(kernel, out_shape=(jax.ShapeDtypeStruct((ROWS, FW), f32),...  1.33 us
    reshape x1, local copies, waits for them, and re-layouts, body(): corr_cols.reshape(1, FW)  1.31 us

profile of v1, /device:TPU:1, one launch (start us, length us, event | category | flops | bytes accessed | tf_op | source)
XLA Modules:
  0.0 38.7 jit_solution(1988432867136656439)
XLA Ops:
  0.6 1.3 %reshape.29.ccol = f32[1,2560]{1,0:T(1,128)} reshape(f32[2560]{0:T(1024)} %param.10) | data formatting | bytes 20480 | tf_op jit(solution)/shard_map/reshape | solution.py:261
  1.9 33.9 %restitch.1 = (f32[16,2560]{1,0:T(8,128)}, f32[1,2560]{1,0:T(1,128)}) custom-call(f32[2,64,2560]{2,1,0:T(8,128)} %res_hbm.1, f32[1,64]{1,0:T(1,128)} %bitcast.11, f32[1,2560]{1,0:T(1,128)} %reshape.29.ccol, s32[1,64]{1,0:T(1,128)} %bitcast.6, s32[1,64]{1,0:T(1,128)} %bitcast.7, s32[1,64]{1,0:T(1,128)} %bitcast.8, s32[1,64]{1,0:T(1,128)} %bitcast.9, ...), custom_call_target="tpu_custom_call" | custom-call | tf_op jit(solution)/shard_map/restitch/pallas_call | solution.py:239
  35.8 1.3 %reduce = f32[2560]{0:T(1024)} reduce(f32[1,2560]{1,0:T(1,128)} %get-tuple-element.5, f32[]{:T(128)} %constant.1), dimensions={0}, to_apply=%get-tuple-element.5.reduce_sub_computation | reduce | bytes 20484 | tf_op jit(solution)/shard_map/restitch/pallas_call | solution.py:239
  37.1 1.6 %copy.11 = f32[16,2560]{1,0:T(8,128)} copy(f32[16,2560]{1,0:T(8,128)} %get-tuple-element.8) | data formatting | bytes 327680

commit v2 on v1

v2 whole, which is shorter than its diff:
```python
import jax
import jax.numpy as jnp
from jax import lax
from jax.experimental import pallas as pl
from jax.experimental.pallas import tpu as pltpu
from jax.sharding import PartitionSpec as P


MESH = pl.DeviceIdType.MESH
FH, FW, SLOTS, ROWS, QUARTER, LANES = 64, 2560, 64, 16, 640, 128
STRIPS, COLS, ZS, XS, TILES = 32, 8, 8, 4, 20
FAR_FIRST = (4, 3, 5, 2, 6, 1, 7, 0)


def squared_sine(position, count):
    return jnp.sin(jnp.pi * ((position.astype(jnp.float32) + 0.5) / count)) ** 2


def parts_of(value):
    first = value.astype(jnp.bfloat16)
    rest = value - first.astype(jnp.float32)
    second = rest.astype(jnp.bfloat16)
    third = (rest - second.astype(jnp.float32)).astype(jnp.bfloat16)
    return first, second, third


def binned(one_hot, upper, value):
    placed = jnp.concatenate([jnp.where(upper, value, 0.0), jnp.where(upper, 0.0, value)], axis=0)
    total = None
    for part in parts_of(placed):
        product = jnp.dot(one_hot, part, preferred_element_type=jnp.float32)
        total = product if total is None else total + product
    return total


def wait_for(ref, sem):
    pltpu.make_async_copy(ref, ref, sem).wait()


def kernel(
    res_hbm, crow_hbm, ccol_hbm, rows_hbm, ints_hbm,
    land, pall,
    data, crow, ccol, ints_v, ints_s, rowfac, colfac, turned, send1, recv1, tile, psum, pgot, psend,
    load_sems, s1, r1, s2, r2, s3, r3, s4, r4,
):
    strip = lax.axis_index("strip")
    col = lax.axis_index("col")
    z, x = strip >> 2, strip & 3
    y, core = col >> 1, col & 1

    def plane():
        for dz in FAR_FIRST:
            for dx in (2, 1, 3, 0):
                if dz or dx:
                    yield ((z + dz) & 7), ((x + dx) & 3)

    barrier = pltpu.get_barrier_semaphore()
    for pz, px in plane():
        pl.semaphore_signal(barrier, inc=1, device_id=((pz << 2) + px, col), device_id_type=MESH)
    for step in range(1, COLS):
        pl.semaphore_signal(barrier, inc=1, device_id=(strip, (col + step) & 7), device_id_type=MESH)

    loads = [pltpu.make_async_copy(h, v, load_sems.at[n]) for n, (h, v) in enumerate(
        [(ints_hbm[k], ints_s.at[k]) for k in range(5)] + [(crow_hbm, crow), (ccol_hbm, ccol)]
        + [(rows_hbm[k], ints_v.at[k]) for k in range(5)] + [(res_hbm, data)]
    )]
    for load in loads:
        load.start()

    diagonal = lax.broadcasted_iota(jnp.int32, (SLOTS, SLOTS), 0) == lax.broadcasted_iota(jnp.int32, (SLOTS, SLOTS), 1)

    def upright(row):
        return jnp.sum(jnp.where(diagonal, row, 0.0), axis=1, keepdims=True)

    row_index = lax.broadcasted_iota(jnp.int32, (FH, LANES), 0)
    row_base = squared_sine(row_index, FH)
    col_base = squared_sine(lax.broadcasted_iota(jnp.int32, (8, FW), 1), FW)
    for load in loads[:-1]:
        load.wait()
    row_base = row_base * upright(crow[...])
    for n in range(TILES):
        part = slice(LANES * n, LANES * (n + 1))
        colfac[:, part] = col_base[:, part] * ccol[n : n + 1, :]
    facets = []
    for i in range(2):
        facet = ints_s[0, 2 * strip + i]
        inside = (row_index >= ints_s[3, facet]) & (row_index < ints_s[4, facet])
        rowfac[i] = jnp.where(inside, row_base, 0.0)
        facets.append((ints_s[1, facet], ints_s[2, facet]))
    loads[-1].wait()

    sub = lax.broadcasted_iota(jnp.int32, (8, LANES), 0)
    lane = lax.broadcasted_iota(jnp.int32, (8, LANES), 1)
    for i in range(2):
        row_anchor, col_anchor = facets[i]
        first_row = (8 * core + 448 - row_anchor) & 63
        first_col = lax.rem(QUARTER * y + 17920 - col_anchor, FW)
        group, row_off = first_row >> 3, first_row & 7
        column, col_off = first_col >> 7, first_col & 127
        row_roll, col_roll = (8 - row_off) & 7, (LANES - col_off) & 127
        in_first_row, in_first_col = sub < 8 - row_off, lane < LANES - col_off
        group, column = jnp.full((8, LANES), group), jnp.full((8, LANES), column)
        for k in range(8):
            row_factor = rowfac[i, 8 * k : 8 * k + 8, :]
            tiles = []
            for n in range(TILES):
                part = pl.ds(LANES * n, LANES)
                tiles.append(data[i, pl.ds(8 * k, 8), part] * (row_factor * colfac[:, part]))
            for bit, count in ((16, 20), (8, 13), (4, 9), (2, 7), (1, 6)):
                moved = (column & bit) != 0
                tiles = [jnp.where(moved, tiles[(n + bit) % len(tiles)], tiles[n]) for n in range(count)]
            tiles = [pltpu.roll(tile_n, col_roll, 1) for tile_n in tiles]
            for n in range(5):
                turned[k, :, LANES * n : LANES * (n + 1)] = jnp.where(in_first_col, tiles[n], tiles[n + 1])
        for n in range(5):
            part = pl.ds(LANES * n, LANES)
            rows = [turned[k, :, part] for k in range(8)]
            for bit in (4, 2, 1):
                moved = (group & bit) != 0
                rows = [jnp.where(moved, rows[(k + bit) % 8], rows[k]) for k in range(8)]
            rows = [pltpu.roll(row_k, row_roll, 0) for row_k in rows]
            for xq in range(XS):
                send1[xq, :, i, part] = jnp.where(in_first_row, rows[2 * xq], rows[2 * xq + 1])

    pl.semaphore_wait(barrier, STRIPS - 1 + COLS - 1)

    for pz, px in plane():
        pltpu.make_async_remote_copy(
            src_ref=send1.at[px, pz], dst_ref=recv1.at[strip], send_sem=s1, recv_sem=r1,
            device_id=((pz << 2) + px, col), device_id_type=MESH,
        ).start()
    pltpu.make_async_copy(send1.at[x, z], recv1.at[strip], r1).start()

    m = 16 * x + 8 * core + z
    facet_of = upright(ints_v[0].astype(jnp.float32)).astype(jnp.int32)
    chosen = facet_of == lax.broadcasted_iota(jnp.int32, (SLOTS, SLOTS), 1)

    def by_slot(row):
        return jnp.sum(jnp.where(chosen, row.astype(jnp.float32), 0.0), axis=1, keepdims=True).astype(jnp.int32)

    ra, ca, vf, ve = (by_slot(ints_v[k]) for k in range(1, 5))
    block = (ra >> 6) + (m < (ra & 63)).astype(jnp.int32)
    facet_row = (m - ra) & 63
    row_weight = jnp.where((facet_row >= vf) & (facet_row < ve), squared_sine(facet_row, FH), 0.0)
    column_group = sum((ca >= FW * k).astype(jnp.int32) for k in range(1, COLS))
    first_class = ca - FW * column_group
    class_index = QUARTER * y + lax.broadcasted_iota(jnp.int32, (SLOTS, QUARTER), 1)
    upper = class_index >= first_class
    facet_col = class_index - first_class + jnp.where(upper, 0, FW)
    weight = row_weight * squared_sine(facet_col, FW)
    wide_lane = lax.broadcasted_iota(jnp.int32, (SLOTS, 2 * SLOTS), 1)
    wide_sub = lax.broadcasted_iota(jnp.int32, (SLOTS, 2 * SLOTS), 0)
    low_bin = (8 * block + column_group).astype(jnp.float32)
    bin_row = jnp.sum(jnp.where((wide_lane & 63) == wide_sub, low_bin, 0.0), axis=0, keepdims=True)
    bin_row = bin_row.astype(jnp.int32) + (wide_lane[:1] >> 6)
    one_hot = (wide_sub == bin_row).astype(jnp.float32).astype(jnp.bfloat16)
    scale = 1.0 / jnp.maximum(binned(one_hot, upper, weight), 0.5)

    wait_for(recv1, r1)
    stitched = binned(one_hot, upper, recv1[...].reshape(SLOTS, QUARTER)) * scale
    squares = stitched * stitched
    sums = squares[0:8]
    for q in range(1, 8):
        sums = sums + squares[8 * q : 8 * q + 8]
    psum[0] = sums[0:4]
    psum[1] = sums[4:8]
    tile[:, 0, :] = stitched

    place = 2 * x + core
    for dx in (2, 1, 3, 0):
        for dc in (1, 0):
            if dx or dc:
                px, pc = (x + dx) & 3, core ^ dc
                pltpu.make_async_remote_copy(
                    src_ref=psum.at[pc], dst_ref=pgot.at[place], send_sem=s3, recv_sem=r3,
                    device_id=((z << 2) + px, 2 * y + pc), device_id_type=MESH,
                ).start()
    pltpu.make_async_copy(psum.at[core], pgot.at[place], r3).start()

    row = 8 * core + z
    cols = pl.ds(pl.multiple_of(QUARTER * y, LANES), QUARTER)
    for dz in FAR_FIRST:
        for dg in (4, 3, 5, 2, 6, 1, 7, 0):
            if dz or dg:
                pz, pg = (z + dz) & 7, (col + dg) & 7
                pltpu.make_async_remote_copy(
                    src_ref=tile.at[(pz << 3) + pg], dst_ref=land.at[row, :, cols], send_sem=s2, recv_sem=r2,
                    device_id=((pz << 2) + x, pg), device_id_type=MESH,
                ).start()
    pltpu.make_async_copy(tile.at[(z << 3) + col], land.at[row, :, cols], r2).start()

    wait_for(pgot, r3)
    total = pgot[0]
    for k in range(1, 8):
        total = total + pgot[k]
    psend[:, 0, :] = total
    own_half = (col >> 2) == core
    for dz in FAR_FIRST:
        for k in range(4):
            def remote():
                pltpu.make_async_remote_copy(
                    src_ref=psend.at[k], dst_ref=pall.at[z, :, cols], send_sem=s4, recv_sem=r4,
                    device_id=((((z + dz) & 7) << 2) + x, 4 * core + k), device_id_type=MESH,
                ).start()

            if dz:
                remote()
            else:
                own = 4 * core + k == col
                pl.when(jnp.logical_not(own))(remote)

                @pl.when(own)
                def _():
                    pltpu.make_async_copy(psend.at[k], pall.at[z, :, cols], r4).start()

    wait_for(recv1.at[pl.ds(0, STRIPS - 1)], s1)
    wait_for(pgot.at[pl.ds(0, 7)], s3)
    wait_for(tile.at[pl.ds(0, 63)], s2)
    wait_for(tile.at[pl.ds(0, 31)], s4)

    @pl.when(jnp.logical_not(own_half))
    def _():
        wait_for(tile.at[0], s4)

    wait_for(land, r2)
    wait_for(pall, r4)


def finish(land, pall, out, power):
    for n in range(TILES):
        part = slice(LANES * n, LANES * (n + 1))
        out[:, part] = land[:, 0, part]
        power[n : n + 1, :] = jnp.sum(pall[:, 0, part], axis=0, keepdims=True) / (FH * 8)


def body(residuals, corr_rows, corr_cols, row_anchor, col_anchor, valid_first, valid_end, facet_of_slot):
    ints = (facet_of_slot, row_anchor, col_anchor, valid_first, valid_end)
    hbm = pl.BlockSpec(memory_space=pl.ANY)
    vmem = pl.BlockSpec(memory_space=pltpu.VMEM)
    f32, i32 = jnp.float32, jnp.int32
    dma = pltpu.SemaphoreType.DMA
    land, pall = pl.pallas_call(
        lambda a, b, c, *refs: kernel(a, b, c, refs[:5], refs[5:10], *refs[10:]),
        out_shape=(pltpu.VMEM((ROWS, 1, FW), f32), pltpu.VMEM((ZS, 1, FW), f32)),
        in_specs=[hbm] * 13,
        out_specs=(vmem, vmem),
        scratch_shapes=[
            pltpu.VMEM((2, FH, FW), f32),
            pltpu.VMEM((1, FH), f32),
            pltpu.VMEM((TILES, LANES), f32),
            pltpu.VMEM((5, 1, SLOTS), i32),
            pltpu.SMEM((5, SLOTS), i32),
            pltpu.VMEM((2, FH, LANES), f32),
            pltpu.VMEM((8, FW), f32),
            pltpu.VMEM((8, 8, QUARTER), f32),
            pltpu.VMEM((XS, ZS, 2, QUARTER), f32),
            pltpu.VMEM((STRIPS, 2, QUARTER), f32),
            pltpu.VMEM((64, 1, QUARTER), f32),
            pltpu.VMEM((2, 4, QUARTER), f32),
            pltpu.VMEM((8, 4, QUARTER), f32),
            pltpu.VMEM((4, 1, QUARTER), f32),
            dma((13,)),
        ]
        + [dma] * 8,
        compiler_params=pltpu.CompilerParams(collective_id=0, has_side_effects=True),
        name="restitch",
    )(
        residuals, corr_rows.reshape(1, FH), corr_cols.reshape(TILES, LANES),
        *(a.reshape(1, SLOTS) for a in ints), *ints,
    )
    stitched, power = pl.pallas_call(
        finish,
        out_shape=(jax.ShapeDtypeStruct((ROWS, FW), f32), jax.ShapeDtypeStruct((TILES, LANES), f32)),
        in_specs=[vmem, vmem],
        out_specs=(vmem, vmem),
        compiler_params=pltpu.CompilerParams(vmem_limit_bytes=4 << 20),
        name="finish",
    )(land, pall)
    return stitched, power.reshape(FW)


def solution(mesh):
    in_specs = (P("strip", None, None), P(), P(), P(), P(), P(), P(), P())
    out_specs = (P("strip", "col"), P("col"))
    return jax.shard_map(body, mesh=mesh, in_specs=in_specs, out_specs=out_specs, check_vma=False)
```

time: 39 us -> 30.3 us (0.78)
  Pallas kernels: 33.9 us -> 29.5 us
  local copies, waits for them, and re-layouts: 2.91 us -> 0 us
  other arithmetic: 1.33 us -> 0 us
    pallas_call x1 -> x2, Pallas kernels: 33.9 us -> 29.5 us  [the longest x1 28.8 us: body(): pl.pallas_call(lambda a, b, c, *refs: kernel(a, b, c, refs[:5], refs[5:10...]
    unnamed x1 -> x0, local copies, waits for them, and re-layouts: 1.59 us -> none
    pallas_call x1 -> x0, other arithmetic: 1.33 us -> none  [body(): pl.pallas_call(kernel, out_shape=(jax.ShapeDtypeStruct((ROWS, FW), f32),...]
    reshape x1 -> x0, local copies, waits for them, and re-layouts: 1.31 us -> none  [body(): corr_cols.reshape(1, FW)]
where the time goes in v2:
time: 30.3 us; the launch traced here: 30.2 us
  Pallas kernels  29.5 us (97%)
  between operations  0.64 us (2%)
    pallas_call x1, Pallas kernels, body(): pl.pallas_call(lambda a, b, c, *refs: kernel(a, b, c, refs[:5], refs[5:10...  28.8 us
    pallas_call x1, Pallas kernels, body(): pl.pallas_call(finish, out_shape=(jax.ShapeDtypeStruct((ROWS, FW), f32),...  0.76 us

profile of v2, /device:TPU:1, one launch (start us, length us, event | category | flops | bytes accessed | tf_op | source)
XLA Modules:
  0.0 30.2 jit_solution(11217807611195929079)
XLA Ops:
  0.6 28.8 %restitch.1 = (f32[16,1,2560]{2,1,0:T(1,128)S(1)}, f32[8,1,2560]{2,1,0:T(1,128)S(1)}) custom-call(f32[2,64,2560]{2,1,0:T(8,128)} %a.1, f32[1,64]{1,0:T(1,128)} %bitcast.14, f32[20,128]{1,0:T(8,128)} %bitcast.8, s32[1,64]{1,0:T(1,128)} %bitcast.9, s32[1,64]{1,0:T(1,128)} %bitcast.10, s32[1,64]{1,0:T(1,128)} %bitcast.11, s32[1,64]{1,0:T(1,128)} %bitcast.12, ...), custom_call_target="tpu_custom_call" | custom-call | tf_op jit(solution)/shard_map/restitch/pallas_call | solution.py:242
  29.4 0.8 %finish.1 = (f32[16,2560]{1,0:T(8,128)}, f32[20,128]{1,0:T(8,128)}) custom-call(f32[16,1,2560]{2,1,0:T(1,128)S(1)} %get-tuple-element.6.land, f32[8,1,2560]{2,1,0:T(1,128)S(1)} %get-tuple-element.7.pall), custom_call_target="tpu_custom_call" | custom-call | tf_op jit(solution)/shard_map/finish/pallas_call | solution.py:271
